TPU v7x, 256 devices: a whole 4x4x8 slice. The times are simulated.
256 devices in a mesh: dp: 16 (over z_hi, x), row: 2 (over z_lo), col: 8 (over y, core).
Axes of the slice: x: 4, y: 4, z: 8 (z_hi: 4, z_lo: 2; z = z_hi * 2 + z_lo), core: 2. Of those that a mesh axis runs over, the one named last changes fastest.
Arguments:
- activations: bfloat16 [16384, 2048], P('dp', ('row', 'col')), may hold values from -0.08984375 to 0.08984375
- gate_input: bfloat16 [16384, 5120], P('dp', ('row', 'col')), may hold values from -6 to 6
- up_input: bfloat16 [16384, 5120], P('dp', ('row', 'col')), may hold values from -6 to 6
- hidden_grad: bfloat16 [16384, 5120], P('dp', ('row', 'col')), may hold values from -6 to 6
- weight_gate: bfloat16 [2048, 5120], P(None, ('row', 'col')), may hold values from -0.125 to 0.125
- weight_up: bfloat16 [2048, 5120], P(None, ('row', 'col')), may hold values from -0.125 to 0.125
Outputs:
- input_grad: float32 [16384, 2048], P('dp', ('row', 'col'))
- gate_weight_grad: float32 [2048, 5120], P(None, ('row', 'col'))
- up_weight_grad: float32 [2048, 5120], P(None, ('row', 'col'))
All inputs are finite; a program needn't handle non-finite values.
Results may differ from a plain program's by a relative error of at most 0.0029.
Values may be sent and summed in bfloat16 or wider, within the bound.
A program may use at most 128 MiB of HBM per device.

v0:
```python
import jax
import jax.numpy as jnp
from jax import lax
from jax.sharding import Mesh
from jax.sharding import PartitionSpec as P

ROW_COL = ("row", "col_0", "col_1")


ROOT_TWO_PI = 0.7978845608028654
CUBIC = 0.044715


def split_up(shard, dim, devices):
    before, after = (shard.shape[:dim], shard.shape[dim + 1 :])
    return jnp.moveaxis(shard.reshape(*before, devices, -1, *after), dim, 0)


def scatter_pairs(shard, chips, core, dim):
    sizes = (lax.axis_size(chips), lax.axis_size(core))
    parts = split_up(shard, dim, sizes[0] * sizes[1])
    inside = parts.shape[1:]
    parts = parts.reshape(*sizes, *inside).swapaxes(0, 1).reshape(-1, *inside)
    parts = lax.psum_scatter(parts, core, scatter_dimension=0, tiled=True)
    return lax.psum_scatter(parts, chips, scatter_dimension=0, tiled=True)[0]


def geglu_grads(gate_input, up_input, hidden_grad):
    gate_pre = gate_input.astype(jnp.float32)
    up_pre = up_input.astype(jnp.float32)
    grad_hidden = hidden_grad.astype(jnp.float32)
    tanh_part = jnp.tanh(ROOT_TWO_PI * (gate_pre + CUBIC * gate_pre * gate_pre * gate_pre))
    gelu_value = 0.5 * gate_pre * (1.0 + tanh_part)
    gelu_slope = 0.5 * (1.0 + tanh_part) + 0.5 * gate_pre * (
        1.0 - tanh_part * tanh_part
    ) * ROOT_TWO_PI * (1.0 + 3.0 * CUBIC * gate_pre * gate_pre)
    gate_grad = (grad_hidden * up_pre * gelu_slope).astype(jnp.bfloat16)
    up_grad = (grad_hidden * gelu_value).astype(jnp.bfloat16)
    return (gate_grad, up_grad)


def contract_hidden(weight_rows, grad_rows):
    return lax.dot_general(
        weight_rows, grad_rows, (((1,), (1,)), ((), ())), preferred_element_type=jnp.float32
    )


def contract_tokens(act_rows, grad_rows):
    return lax.dot_general(
        act_rows, grad_rows, (((0,), (0,)), ((), ())), preferred_element_type=jnp.float32
    )


def body(activations, gate_input, up_input, hidden_grad, weight_gate, weight_up):
    gate_grad, up_grad = geglu_grads(gate_input, up_input, hidden_grad)
    hidden_part = gate_grad.shape[1]
    both_grads = jnp.concatenate([gate_grad, up_grad], axis=1)
    gathered = lax.all_gather(activations, ROW_COL, axis=1, tiled=True)
    stacked = contract_tokens(gathered, both_grads)
    gate_weight_grad, up_weight_grad = lax.psum(
        (stacked[:, :hidden_part], stacked[:, hidden_part:]), "dp"
    )
    input_cols = scatter_pairs(
        contract_hidden(weight_gate, gate_grad) + contract_hidden(weight_up, up_grad),
        ("row", "col_0"),
        "col_1",
        0,
    )
    input_grad = jnp.transpose(input_cols)
    return (input_grad, gate_weight_grad, up_weight_grad)


def solution(mesh):
    split = Mesh(
        mesh.devices.reshape(mesh.shape["dp"], mesh.shape["row"], 4, 2),
        ("dp", "row", "col_0", "col_1"),
    )
    in_specs = (
        P("dp", ROW_COL),
        P("dp", ROW_COL),
        P("dp", ROW_COL),
        P("dp", ROW_COL),
        P(None, ROW_COL),
        P(None, ROW_COL),
    )
    out_specs = (P("dp", ROW_COL), P(None, ROW_COL), P(None, ROW_COL))
    return jax.shard_map(body, mesh=split, in_specs=in_specs, out_specs=out_specs, check_vma=False)
```

profile of v0, /device:TPU:2, one launch (start us, length us, event | category | flops | bytes accessed | tf_op | source)
XLA Modules:
  0.0 372.6 jit_solution(16325375190990961636)
XLA Ops:
  8.0 0.0 copy-start
  8.0 0.0 all-gather.2.cloned.1.call-start
  8.1 0.7 all-gather.2.cloned.1.call-update
  8.7 0.0 reduce-scatter.3.cloned.1.call-start
  8.8 2.6 fusion.7
  11.4 0.0 copy-done
  11.4 0.0 copy-start.3
  11.4 2.4 fusion.16
  13.8 5.8 %add_bitcast_fusion = f32[2048,1024]{0,1:T(8,128)} fusion(f32[1024,2048]{1,0:T(8,128)S(1)} %fusion.16, bf16[1024,320]{0,1:T(8,128)(2,1)S(1)} %get-tuple-element.7, bf16[2048,320]{0,1:T(8,128)(2,1)S(1)} %copy-done.3), kind=kOutput, calls=%fused_computation | convolution fusion | flops 1344274432 | bytes 18743296 | tf_op jit(solution)/shard_map/dot_general | solution.py:43
  19.6 11.7 %reshape_reshape.3 = f32[8,2,128,1024]{2,1,0,3:T(2,128)} reshape(f32[2048,1024]{0,1:T(8,128)} %add_bitcast_fusion) | data formatting | bytes 16777216 | tf_op jit(solution)/shard_map/reshape;reshape | solution.py:23
  31.4 9.3 %copy.9 = f32[2,8,128,1024]{2,3,1,0:T(8,128)} copy(f32[2,8,128,1024]{2,0,1,3:T(2,128)} %bitcast.17) | data formatting | bytes 16777216 | tf_op jit(solution)/shard_map/transpose | solution.py:23
  40.7 0.0 reduce-scatter.3.cloned.1.call-update
  40.7 0.0 all-reduce.3.cloned.1.call-start
  40.8 20.7 %all-gather.2.cloned.1.call-done = bf16[1024,2048]{1,0:T(8,128)(2,1)} async-done(((bf16[1024,128]{1,0:T(8,128)(2,1)}), bf16[1024,2048]{1,0:T(8,128)(2,1)}) %all-gather.2.cloned.1.call-update) | async-done | bytes 4194320 | tf_op jit(solution)/shard_map/all_gather | solution.py:58
  61.5 5.3 %convolution_bitcast_fusion = f32[2048,640]{0,1:T(8,128)S(1)} fusion(bf16[1024,2048]{1,0:T(8,128)(2,1)} %all-gather.2.cloned.1.call-done, bf16[1024,320]{0,1:T(8,128)(2,1)S(1)} %get-tuple-element.7, bf16[1024,320]{0,1:T(8,128)(2,1)S(1)} %get-tuple-element.8), kind=kOutput, calls=%fused_computation.1 | convolution fusion | flops 2686976000 | bytes 10747904 | tf_op jit(solution)/shard_map/dot_general | solution.py:49
  66.7 3.0 fusion.15
  69.7 0.0 all-reduce.3.cloned.1.call-update
  69.8 0.0 reduce-scatter.5.cloned.1.call-start
  69.8 0.0 reduce-scatter.3.cloned.1.call-done
  69.8 0.5 reduce-scatter.5.cloned.1.call-update
  70.3 288.9 %all-reduce.3.cloned.1.call-done = (f32[2048,320]{0,1:T(8,128)}, f32[2048,320]{0,1:T(8,128)}) async-done(((f32[2048,320]{0,1:T(8,128)}, f32[2048,320]{0,1:T(8,128)}), (f32[2048,320]{0,1:T(8,128)}, f32[2048,320]{0,1:T(8,128)})) %all-reduce.3.cloned.1.call-update) | async-done | bytes 5242896 | tf_op jit(solution)/shard_map/psum | solution.py:60
  359.2 3.7 copy.12
  362.9 1.5 copy.13
  364.4 0.8 copy-done.1
  (5 shorter events, 0.0 us)
Async XLA Ops:
  8.0 3.4 copy-start
  8.0 53.4 %all-gather.2.cloned.1.call-start = ((), (), s32[]{:S(2)}) async-start(), calls=%async_computation.4 | async-start | bytes 4456448 | tf_op jit(solution)/shard_map/all_gather | solution.py:58
  8.7 61.1 %reduce-scatter.3.cloned.1.call-start = ((), (), s32[]{:S(2)}) async-start(), calls=%async_computation.2 | async-start | bytes 12582912 | tf_op jit(solution)/shard_map/reduce_scatter | solution.py:24
  11.4 2.4 copy-start.3
  40.7 318.5 %all-reduce.3.cloned.1.call-start = ((), (), s32[]{:S(2)}) async-start(), calls=%async_computation.5 | async-start | bytes 10485760 | tf_op jit(solution)/shard_map/psum | solution.py:60
  69.8 289.4 %reduce-scatter.5.cloned.1.call-start = ((), (), s32[]{:S(2)}) async-start(), calls=%async_computation.3 | async-start | bytes 4718592 | tf_op jit(solution)/shard_map/reduce_scatter | solution.py:25
  359.2 3.7 copy-start.2
  362.9 2.3 copy-start.1
Sparse Core Ops, SparseCore 0:
  10.6 50.8 all-gather.1
  69.9 289.2 all-reduce.2
Sparse Core Ops, SparseCore 1:
  40.8 24.9 reduce-scatter.2
  73.4 56.0 reduce-scatter.4
where the time goes:
time: 379 us; the launch traced here: 373 us
  waiting for transfers between devices  311 us (82%)
  local copies, waits for them, and re-layouts  30 us (8%)
  between operations  15.5 us (4%)
  matrix products  13.5 us (4%)
    psum x1, waiting for transfers between devices, body(): lax.psum((stacked[:, :hidden_part], stacked[:, hidden_part:]), 'dp')  289 us
    all_gather x1, waiting for transfers between devices, body(): gathered = lax.all_gather(activations, ROW_COL, axis=1, tiled=True)  20.7 us
    another operation x1, local copies, waits for them, and re-layouts, scatter_pairs(): parts = parts.reshape(*sizes, *inside).swapaxes(0, 1).reshape(-1, *inside)  11.7 us
    transpose x1, local copies, waits for them, and re-layouts, scatter_pairs(): parts = parts.reshape(*sizes, *inside).swapaxes(0, 1).reshape(-1, *inside)  9.33 us
    dot_general x2, matrix products, contract_hidden(): lax.dot_general(weight_rows, grad_rows, (((1,), (1,)), ((), ())), preferr...  8.19 us
  transfers between devices with their start and end apart: 4, of which 2 were waited for; matrix products, arithmetic and copies ran while one was open for 11% of the time, Pallas kernels for 0%

commit v1 on v0

v1 whole, which is shorter than its diff:
```python
import functools

import jax
import jax.numpy as jnp
from jax import lax
from jax.experimental import pallas as pl
from jax.experimental.pallas import tpu as pltpu
from jax.sharding import PartitionSpec as P

ROOT_TWO_PI = 0.7978845608028654
CUBIC = 0.044715
MESH = pl.DeviceIdType.MESH
F32, BF16 = jnp.float32, jnp.bfloat16

TOK = 1024
HID = 320
WIDE = 2 * HID
COLS = 128
D = 2048
CHUNKS = 8
CH = D // CHUNKS
XR = CH // 4
ZR = XR // 4
NT = (((1,), (1,)), ((), ()))


def geglu_grads(gate_input, up_input, hidden_grad):
    gate_pre = gate_input.astype(F32)
    up_pre = up_input.astype(F32)
    grad_hidden = hidden_grad.astype(F32)
    tanh_part = jnp.tanh(ROOT_TWO_PI * (gate_pre + CUBIC * gate_pre * gate_pre * gate_pre))
    gelu_value = 0.5 * gate_pre * (1.0 + tanh_part)
    gelu_slope = 0.5 * (1.0 + tanh_part) + 0.5 * gate_pre * (
        1.0 - tanh_part * tanh_part
    ) * ROOT_TWO_PI * (1.0 + 3.0 * CUBIC * gate_pre * gate_pre)
    return (grad_hidden * up_pre * gelu_slope).astype(BF16), (grad_hidden * gelu_value).astype(BF16)


def store_packed(ref, rows, first, second):
    ref[rows, 0:256] = first[:, 0:256]
    ref[rows, 256:512] = second[:, 0:256]
    ref[rows, 512:640] = jnp.concatenate([first[:, 256:320], second[:, 256:320]], axis=1)


def kernel(
    act_h, gate_h, up_h, hid_h, wg_h, wu_h,
    w_out, own_out, last_out,
    act_v, gate_v, up_v, hid_v, wg_v, wu_v, wp, gp, ag,
    part, xs, xr, x3, qs, q1, zr, z3, z3r,
    pkeep, bs, br, ykeep, ys, yr, y3, tz,
    in_sem, ag_recv, ag_send, c_recv, c_send, b_recv, b_send, y_recv, y_send, t_recv, t_send,
):
    dp, row, col = lax.axis_index("dp"), lax.axis_index("row"), lax.axis_index("col")
    zh, x = dp // 4, lax.rem(dp, 4)
    y, core = col // 2, lax.rem(col, 2)
    s = 2 * core - 1

    def at(base, step):
        return lax.rem(base + step + 4, 4)

    def dev(dx=0, dzh=0, dy=0, flip_row=False, flip_core=False):
        return (
            at(zh, dzh) * 4 + at(x, dx),
            1 - row if flip_row else row,
            at(y, dy) * 2 + (1 - core if flip_core else core),
        )

    x_up, x_down = dev(dx=s), dev(dx=-s)
    z_up, z_down = dev(dzh=s), dev(dzh=-s)
    y_up, y_down = dev(dy=s), dev(dy=-s)
    pair, mate = dev(flip_row=True), dev(flip_core=True)

    loads = []
    for n, (src, dst) in enumerate(
        ((act_h, act_v), (gate_h, gate_v), (up_h, up_v), (hid_h, hid_v), (wg_h, wg_v), (wu_h, wu_v))
    ):
        loads.append(pltpu.make_async_copy(src, dst, in_sem.at[n]))
        loads[-1].start()

    barrier = pltpu.get_barrier_semaphore()
    for other in (x_up, x_down, z_up, z_down, y_up, y_down, pair, mate):
        pl.semaphore_signal(barrier, inc=1, device_id=other, device_id_type=MESH)

    sent = []

    def send(src, dst, send_sem, recv_sem, to):
        copy = pltpu.make_async_remote_copy(
            src_ref=src, dst_ref=dst, send_sem=send_sem, recv_sem=recv_sem,
            device_id=to, device_id_type=MESH,
        )
        copy.start()
        sent.append(copy)

    def arrived(dst, recv_sem, send_sem):
        pltpu.make_async_remote_copy(
            src_ref=dst, dst_ref=dst, send_sem=send_sem, recv_sem=recv_sem,
            device_id=mate, device_id_type=MESH,
        ).wait_recv()

    def place(other_row, dy, other_core=False):
        return (1 - row if other_row else row) * 8 + at(y, dy) * 2 + (1 - core if other_core else core)

    n_ag = [0]

    def ag_give(slot, to):
        send(ag.at[slot], ag.at[slot], ag_send.at[n_ag[0]], ag_recv.at[slot], to)
        n_ag[0] += 1

    def ag_take(slot):
        arrived(ag.at[slot], ag_recv.at[slot], ag_send.at[0])

    own = place(False, 0)
    loads[0].wait()
    ag[own] = act_v[...].T
    pl.semaphore_wait(barrier, 8)
    for to in (pair, y_up, y_down, mate):
        ag_give(own, to)

    for load in loads[1:4]:
        load.wait()

    def gate_rows(i, carry):
        rows = pl.ds(pl.multiple_of(i * 64, 64), 64)
        store_packed(gp, rows, *geglu_grads(gate_v[rows, :], up_v[rows, :], hid_v[rows, :]))
        return carry

    lax.fori_loop(0, TOK // 64, gate_rows, 0)

    order = ((False, 0), (True, 0), (False, -s), (False, s), (True, -s), (True, s), (False, 2), (True, 2))

    def base_row(k):
        other_row, dy = order[k]
        return pl.multiple_of(((1 - row if other_row else row) * 8 + at(y, dy) * 2) * COLS, CH)

    def c_give(k, n, src, dst, to):
        send(src, dst, c_send.at[k, n], c_recv.at[k, n], to)

    def c_take(k, n, dst):
        arrived(dst, c_recv.at[k, n], c_send.at[k, n])

    def x_rows(place_x):
        return pl.ds(pl.multiple_of(place_x * XR, XR), XR)

    def c0(k):
        other_row, dy = order[k]
        ag_take(place(other_row, dy, True))
        first = pl.multiple_of(place(other_row, dy) - core, 2)
        lhs = ag[pl.ds(first, 2)].reshape(CH, TOK)
        part[k] = jnp.dot(lhs, gp[...], preferred_element_type=F32)
        xs[k, 0] = part[k, x_rows(at(x, 2)), :].astype(BF16)
        c_give(k, 0, xs.at[k, 0], xr.at[k, 0], x_up)
        xs[k, 1] = part[k, x_rows(at(x, -s)), :].astype(BF16)
        c_give(k, 1, xs.at[k, 1], xr.at[k, 1], x_down)

    def c1(k):
        c_take(k, 0, xr.at[k, 0])
        x3[k] = (part[k, x_rows(at(x, s)), :] + xr[k, 0].astype(F32)).astype(BF16)
        c_give(k, 2, x3.at[k], xr.at[k, 2], x_up)

    def c2(k):
        c_take(k, 1, xr.at[k, 1])
        c_take(k, 2, xr.at[k, 2])
        q1[k] = part[k, x_rows(x), :] + xr[k, 1].astype(F32) + xr[k, 2].astype(F32)
        qs[k, 0] = q1[k, z_rows(at(zh, 2)), :].astype(BF16)
        c_give(k, 3, qs.at[k, 0], zr.at[k, 0], z_up)
        qs[k, 1] = q1[k, z_rows(at(zh, -s)), :].astype(BF16)
        c_give(k, 4, qs.at[k, 1], zr.at[k, 1], z_down)

    def z_rows(place_z):
        return pl.ds(pl.multiple_of(place_z * ZR, ZR), ZR)

    def c3(k):
        c_take(k, 3, zr.at[k, 0])
        z3[k] = q1[k, z_rows(at(zh, s)), :] + zr[k, 0].astype(F32)
        c_give(k, 5, z3.at[k], z3r.at[k], z_up)

    def out_x(k, place_x):
        return w_out.at[pl.ds(pl.multiple_of(base_row(k) + place_x * XR, XR), XR), :]

    def out_z(k, place_z):
        return w_out.at[pl.ds(pl.multiple_of(base_row(k) + x * XR + place_z * ZR, ZR), ZR), :]

    def c4(k):
        c_take(k, 4, zr.at[k, 1])
        c_take(k, 5, z3r.at[k])
        total = q1[k, z_rows(zh), :] + zr[k, 1].astype(F32) + z3r[k]
        mine = out_z(k, zh)
        mine[...] = total.astype(BF16)
        c_give(k, 6, mine, mine, z_up)
        c_give(k, 7, mine, mine, z_down)

    def c5(k):
        got = out_z(k, at(zh, -s))
        c_take(k, 6, got)
        c_give(k, 8, got, got, z_up)

    def c6(k):
        c_take(k, 7, out_z(k, at(zh, s)))
        c_take(k, 8, out_z(k, at(zh, 2)))
        mine = out_x(k, x)
        c_give(k, 9, mine, mine, x_up)
        c_give(k, 10, mine, mine, x_down)

    def c7(k):
        got = out_x(k, at(x, -s))
        c_take(k, 9, got)
        c_give(k, 11, got, got, x_up)

    def c8(k):
        c_take(k, 10, out_x(k, at(x, s)))
        c_take(k, 11, out_x(k, at(x, 2)))

    def ag_pair():
        slot = place(True, 0)
        ag_take(slot)
        for to in (y_up, y_down, mate):
            ag_give(slot, to)

    def ag_near(other_row):
        slot = place(other_row, -s)
        ag_take(slot)
        ag_give(slot, y_up)
        ag_give(slot, mate)
        slot = place(other_row, s)
        ag_take(slot)
        ag_give(slot, mate)

    def ag_far(other_row):
        slot = place(other_row, 2)
        ag_take(slot)
        ag_give(slot, mate)

    def pack_weights():
        loads[4].wait()
        loads[5].wait()

        def step(i, carry):
            rows = pl.ds(pl.multiple_of(i * 128, 128), 128)
            store_packed(wp, rows, wg_v[rows, :], wu_v[rows, :])
            return carry

        lax.fori_loop(0, D // 128, step, 0)

    def b0(i):
        first = ((i // 4) * 8 + at(y, i % 4) * 2) * COLS
        mine = wp[pl.ds(pl.multiple_of(first + core * COLS, COLS), COLS), :]
        others = wp[pl.ds(pl.multiple_of(first + (1 - core) * COLS, COLS), COLS), :]
        both = jnp.concatenate([mine, others], axis=0)

        def step(r, carry):
            rows = pl.ds(pl.multiple_of(r * 256, 256), 256)
            sums = lax.dot_general(gp[rows, :], both, NT, preferred_element_type=F32)
            pkeep[i, rows, :] = sums[:, 0:COLS]
            bs[i, rows, :] = sums[:, COLS : 2 * COLS].astype(BF16)
            return carry

        lax.fori_loop(0, TOK // 256, step, 0)
        send(bs.at[i], br.at[i], b_send.at[i], b_recv.at[i], mate)

    def b1(r):
        for i in range(4 * r, 4 * r + 4):
            arrived(br.at[i], b_recv.at[i], b_send.at[i])

        def pair_sum(off):
            i = 4 * r + at(0, off)
            return pkeep[i] + br[i].astype(F32)

        ys[r, 0] = pair_sum(2).astype(BF16)
        send(ys.at[r, 0], yr.at[r, 0], y_send.at[r, 0], y_recv.at[r, 0], y_up)
        ys[r, 1] = pair_sum(-s).astype(BF16)
        send(ys.at[r, 1], yr.at[r, 1], y_send.at[r, 1], y_recv.at[r, 1], y_down)
        ykeep[r, 0] = pair_sum(s)
        ykeep[r, 1] = pair_sum(0)

    def b2(r):
        arrived(yr.at[r, 0], y_recv.at[r, 0], y_send.at[r, 0])
        y3[r] = (ykeep[r, 0] + yr[r, 0].astype(F32)).astype(BF16)
        send(y3.at[r], yr.at[r, 2], y_send.at[r, 2], y_recv.at[r, 2], y_up)

    def b3():
        for r in range(2):
            for n in (1, 2):
                arrived(yr.at[r, n], y_recv.at[r, n], y_send.at[r, n])

        def total(r):
            return ykeep[r, 1] + yr[r, 1].astype(F32) + yr[r, 2].astype(F32)

        tz[...] = total(1 - row).astype(BF16)
        send(tz, last_out, t_send, t_recv, pair)
        own_out[...] = total(row)

    def b4():
        arrived(last_out, t_recv, t_send)

    extra = {
        0: (pack_weights, lambda: b0(0), lambda: b0(1), lambda: b0(2), lambda: b0(3), ag_pair),
        1: (lambda: ag_near(False), lambda: b0(4), lambda: b0(5)),
        2: (lambda: b0(6), lambda: b0(7)),
        3: (),
        4: (lambda: ag_near(True),),
        5: (lambda: b1(0), lambda: b1(1)),
        6: (lambda: ag_far(False),),
        7: (lambda: ag_far(True),),
        8: (lambda: b2(0), lambda: b2(1)),
        12: (b3,),
    }
    stages = (c0, c1, c2, c3, c4, c5, c6, c7, c8)
    before = {2, 4, 6, 7}
    for t in range(CHUNKS + len(stages) - 1):
        if t in before:
            for f in extra.get(t, ()):
                f()
        for n in range(len(stages) - 1, -1, -1):
            if 0 <= t - n < CHUNKS:
                stages[n](t - n)
        if t not in before:
            for f in extra.get(t, ()):
                f()
    b4()
    for copy in sent:
        copy.wait_send()


def exchange(*args):
    vmem = pltpu.VMEM
    dma = pltpu.SemaphoreType.DMA
    return pl.pallas_call(
        kernel,
        name="exchange",
        out_shape=(
            jax.ShapeDtypeStruct((D, WIDE), BF16),
            jax.ShapeDtypeStruct((TOK, COLS), F32),
            jax.ShapeDtypeStruct((TOK, COLS), BF16),
        ),
        in_specs=[pl.BlockSpec(memory_space=pl.ANY)] * 6,
        out_specs=[pl.BlockSpec(memory_space=pltpu.VMEM)] * 3,
        scratch_shapes=[
            vmem((TOK, COLS), BF16), vmem((TOK, HID), BF16), vmem((TOK, HID), BF16), vmem((TOK, HID), BF16),
            vmem((D, HID), BF16), vmem((D, HID), BF16), vmem((D, WIDE), BF16), vmem((TOK, WIDE), BF16),
            vmem((16, COLS, TOK), BF16),
            vmem((CHUNKS, CH, WIDE), F32), vmem((CHUNKS, 2, XR, WIDE), BF16), vmem((CHUNKS, 3, XR, WIDE), BF16),
            vmem((CHUNKS, XR, WIDE), BF16), vmem((CHUNKS, 2, ZR, WIDE), BF16), vmem((CHUNKS, XR, WIDE), F32),
            vmem((CHUNKS, 2, ZR, WIDE), BF16), vmem((CHUNKS, ZR, WIDE), F32), vmem((CHUNKS, ZR, WIDE), F32),
            vmem((8, TOK, COLS), F32), vmem((8, TOK, COLS), BF16), vmem((8, TOK, COLS), BF16),
            vmem((2, 2, TOK, COLS), F32), vmem((2, 2, TOK, COLS), BF16), vmem((2, 3, TOK, COLS), BF16),
            vmem((2, TOK, COLS), BF16), vmem((TOK, COLS), BF16),
            dma((6,)), dma((16,)), dma((16,)), dma((CHUNKS, 12)), dma((CHUNKS, 12)), dma((8,)), dma((8,)),
            dma((2, 3)), dma((2, 3)), dma, dma,
        ],
        compiler_params=pltpu.CompilerParams(
            collective_id=0, has_side_effects=True, vmem_limit_bytes=63 * 1024 * 1024
        ),
        cost_estimate=pl.CostEstimate(flops=5 * 10**9, bytes_accessed=10**7, transcendentals=0),
    )(*args)


def finish_kernel(w_ref, own_ref, last_ref, x_ref, gate_ref, up_ref):
    w = w_ref[...].astype(F32)
    gate_ref[:, 0:256] = w[:, 0:256]
    up_ref[:, 0:256] = w[:, 256:512]
    gate_ref[:, 256:320] = w[:, 512:576]
    up_ref[:, 256:320] = w[:, 576:640]
    x_ref[...] = own_ref[...] + last_ref[...].astype(F32)


def finish(w, own, last):
    steps = 8
    return pl.pallas_call(
        finish_kernel,
        name="finish",
        grid=(steps,),
        out_shape=(
            jax.ShapeDtypeStruct((TOK, COLS), F32),
            jax.ShapeDtypeStruct((D, HID), F32),
            jax.ShapeDtypeStruct((D, HID), F32),
        ),
        in_specs=[
            pl.BlockSpec((D // steps, WIDE), lambda i: (i, 0)),
            pl.BlockSpec((TOK // steps, COLS), lambda i: (i, 0)),
            pl.BlockSpec((TOK // steps, COLS), lambda i: (i, 0)),
        ],
        out_specs=(
            pl.BlockSpec((TOK // steps, COLS), lambda i: (i, 0)),
            pl.BlockSpec((D // steps, HID), lambda i: (i, 0)),
            pl.BlockSpec((D // steps, HID), lambda i: (i, 0)),
        ),
        cost_estimate=pl.CostEstimate(flops=10**7, bytes_accessed=10**7, transcendentals=0),
    )(w, own, last)


def body(*args):
    return finish(*exchange(*args))


def solution(mesh):
    spread = ("row", "col")
    in_specs = (P("dp", spread),) * 4 + (P(None, spread),) * 2
    out_specs = (P("dp", spread), P(None, spread), P(None, spread))
    return jax.shard_map(body, mesh=mesh, in_specs=in_specs, out_specs=out_specs, check_vma=False)
```

time: 379 us -> 110 us (0.29); the launches traced: 373 us -> 109 us
  waiting for transfers between devices: 311 us -> 0 us
  Pallas kernels: 0 us -> 93.9 us
  local copies, waits for them, and re-layouts: 30 us -> 14.8 us
  between operations: 15.5 us -> 0.66 us
  matrix products: 13.5 us -> 0 us
    psum x1 -> x0, waiting for transfers between devices: 289 us -> none  [body(): lax.psum((stacked[:, :hidden_part], stacked[:, hidden_part:]), 'dp')]
    pallas_call x0 -> x2, Pallas kernels: none -> 93.9 us  [the longest x1 87.2 us: exchange(): pl.pallas_call(kernel, name='exchange', out_shape=(jax.ShapeDtypeStruct((...]
    all_gather x1 -> x0, waiting for transfers between devices: 20.7 us -> none  [body(): gathered = lax.all_gather(activations, ROW_COL, axis=1, tiled=True)]
    dot_general x3 -> x0, matrix products: 13.5 us -> none  [the longest x2 8.19 us: contract_hidden(): lax.dot_general(weight_rows, grad_rows, (((1,), (1,)), ((), ())), preferr...]
    another operation x1 -> x0, local copies, waits for them, and re-layouts: 11.7 us -> none  [scatter_pairs(): parts = parts.reshape(*sizes, *inside).swapaxes(0, 1).reshape(-1, *inside)]
    transpose x1 -> x0, local copies, waits for them, and re-layouts: 9.33 us -> none  [scatter_pairs(): parts = parts.reshape(*sizes, *inside).swapaxes(0, 1).reshape(-1, *inside)]
    pallas_call x0 -> x2, local copies, waits for them, and re-layouts: none -> 5.74 us  [finish(): pl.pallas_call(finish_kernel, name='finish', grid=(steps,), out_shape=(ja...]
    unnamed x10 -> x13, local copies, waits for them, and re-layouts: 5.97 us -> 9.03 us
  transfers between devices with their start and end apart: 4 -> 0, of which waited for: 2 -> 0; matrix products, arithmetic and copies ran while one was open for 11% -> 0% of each run, Pallas kernels for 0% -> 0%
where the time goes in v1:
time: 110 us; the launch traced here: 109 us
  Pallas kernels  93.9 us (85%)
  local copies, waits for them, and re-layouts  14.8 us (13%)
    pallas_call x1, Pallas kernels, exchange(): pl.pallas_call(kernel, name='exchange', out_shape=(jax.ShapeDtypeStruct((...  87.2 us
    unnamed x13, local copies, waits for them, and re-layouts  9.03 us
    pallas_call x1, Pallas kernels, finish(): pl.pallas_call(finish_kernel, name='finish', grid=(steps,), out_shape=(ja...  6.75 us
    pallas_call x2, local copies, waits for them, and re-layouts, finish(): pl.pallas_call(finish_kernel, name='finish', grid=(steps,), out_shape=(ja...  5.74 us

profile of v1, /device:TPU:2, one launch (start us, length us, event | category | flops | bytes accessed | tf_op | source)
XLA Modules:
  0.0 109.4 jit_solution(1073289654998867133)
XLA Ops:
  0.6 0.0 copy-start.1
  0.6 0.0 copy-start.3
  0.7 2.4 %copy.9.gate_h = bf16[1024,320]{1,0:T(8,128)(2,1)} copy(bf16[1024,320]{0,1:T(8,128)(2,1)} %param.7) | data formatting | bytes 1310720 | tf_op args[1]
  3.0 0.0 copy-start.2
  3.0 2.4 %copy.10.up_h = bf16[1024,320]{1,0:T(8,128)(2,1)} copy(bf16[1024,320]{0,1:T(8,128)(2,1)} %param.8) | data formatting | bytes 1310720 | tf_op args[2]
  5.4 0.0 copy-done.3
  5.4 1.2 %copy.11.hid_h = bf16[1024,320]{1,0:T(8,128)(2,1)} copy(bf16[1024,320]{0,1:T(8,128)(2,1)S(1)} %copy-done.3) | data formatting | bytes 1310720 | tf_op args[3]
  6.6 0.0 copy-done.1
  6.6 1.5 %copy.12.wg_h = bf16[2048,320]{1,0:T(8,128)(2,1)} copy(bf16[2048,320]{0,1:T(8,128)(2,1)S(1)} %copy-done.1) | data formatting | bytes 2621440 | tf_op args[4]
  8.1 0.0 copy-done.2
  8.1 1.5 %copy.13.wu_h = bf16[2048,320]{1,0:T(8,128)(2,1)} copy(bf16[2048,320]{0,1:T(8,128)(2,1)S(1)} %copy-done.2) | data formatting | bytes 2621440 | tf_op args[5]
  9.7 87.2 %exchange.1 = (bf16[2048,640]{1,0:T(8,128)(2,1)}, f32[1024,128]{1,0:T(8,128)}, bf16[1024,128]{1,0:T(8,128)(2,1)}) custom-call(bf16[1024,128]{1,0:T(8,128)(2,1)} %act_h.1, bf16[1024,320]{1,0:T(8,128)(2,1)} %copy.9.gate_h, bf16[1024,320]{1,0:T(8,128)(2,1)} %copy.10.up_h, bf16[1024,320]{1,0:T(8,128)(2,1)} %copy.11.hid_h, bf16[2048,320]{1,0:T(8,128)(2,1)} %copy.12.wg_h, ...), custom_call_target="tpu_custom_call" | custom-call | flops 5000000000 | bytes 10000000 | tf_op jit(solution)/shard_map/exchange/pallas_call | solution.py:327
  96.9 6.7 %finish.1 = (f32[1024,128]{1,0:T(8,128)}, f32[2048,320]{1,0:T(8,128)}, f32[2048,320]{1,0:T(8,128)}) custom-call(bf16[2048,640]{1,0:T(8,128)(2,1)} %get-tuple-element.6.w_ref, f32[1024,128]{1,0:T(8,128)} %get-tuple-element.7.own_ref, bf16[1024,128]{1,0:T(8,128)(2,1)} %get-tuple-element.8.last_ref), custom_call_target="tpu_custom_call" | custom-call | flops 10000000 | bytes 10000000 | tf_op jit(solution)/shard_map/finish/pallas_call | solution.py:368
  103.6 0.0 copy-start
  103.6 3.5 %copy.14 = f32[2048,320]{0,1:T(8,128)} copy(f32[2048,320]{1,0:T(8,128)} %get-tuple-element.10) | data formatting | bytes 5242880 | tf_op jit(solution)/shard_map/finish/pallas_call | solution.py:368
  107.2 0.0 copy-done
  107.2 2.2 %copy.15 = f32[2048,320]{0,1:T(8,128)} copy(f32[2048,320]{1,0:T(8,128)S(1)} %copy-done) | data formatting | bytes 5242880 | tf_op jit(solution)/shard_map/finish/pallas_call | solution.py:368
Async XLA Ops:
  0.6 6.0 %copy-start.1 = (bf16[2048,320]{0,1:T(8,128)(2,1)S(1)}, bf16[2048,320]{0,1:T(8,128)(2,1)}, u32[]{:S(2)}) copy-start(bf16[2048,320]{0,1:T(8,128)(2,1)} %param.10) | copy-start | bytes 3932164
  0.6 4.8 %copy-start.3 = (bf16[1024,320]{0,1:T(8,128)(2,1)S(1)}, bf16[1024,320]{0,1:T(8,128)(2,1)}, u32[]{:S(2)}) copy-start(bf16[1024,320]{0,1:T(8,128)(2,1)} %param.9) | copy-start | bytes 1966084
  3.0 5.1 %copy-start.2 = (bf16[2048,320]{0,1:T(8,128)(2,1)S(1)}, bf16[2048,320]{0,1:T(8,128)(2,1)}, u32[]{:S(2)}) copy-start(bf16[2048,320]{0,1:T(8,128)(2,1)} %param.11) | copy-start | bytes 3932164
  103.6 3.5 %copy-start = (f32[2048,320]{1,0:T(8,128)S(1)}, f32[2048,320]{1,0:T(8,128)}, u32[]{:S(2)}) copy-start(f32[2048,320]{1,0:T(8,128)} %get-tuple-element.11) | copy-start | bytes 7864324

commit v2 on v1

--- a/solution.py
+++ b/solution.py
@@ -18,10 +18,8 @@
 COLS = 128
 D = 2048
 CHUNKS = 8
-CH = D // CHUNKS
-XR = CH // 4
-ZR = XR // 4
-NT = (((1,), (1,)), ((), ()))
+XR = WIDE // 4
+ZR = XR // 2
 
 
 def geglu_grads(gate_input, up_input, hidden_grad):
@@ -36,16 +34,10 @@
     return (grad_hidden * up_pre * gelu_slope).astype(BF16), (grad_hidden * gelu_value).astype(BF16)
 
 
-def store_packed(ref, rows, first, second):
-    ref[rows, 0:256] = first[:, 0:256]
-    ref[rows, 256:512] = second[:, 0:256]
-    ref[rows, 512:640] = jnp.concatenate([first[:, 256:320], second[:, 256:320]], axis=1)
-
-
 def kernel(
     act_h, gate_h, up_h, hid_h, wg_h, wu_h,
     w_out, own_out, last_out,
-    act_v, gate_v, up_v, hid_v, wg_v, wu_v, wp, gp, ag,
+    gate_v, up_v, hid_v, wp, gp_t, gp, ag,
     part, xs, xr, x3, qs, q1, zr, z3, z3r,
     pkeep, bs, br, ykeep, ys, yr, y3, tz,
     in_sem, ag_recv, ag_send, c_recv, c_send, b_recv, b_send, y_recv, y_send, t_recv, t_send,
@@ -70,9 +62,16 @@
     y_up, y_down = dev(dy=s), dev(dy=-s)
     pair, mate = dev(flip_row=True), dev(flip_core=True)
 
+    def place(other_row, dy, other_core=False):
+        return (1 - row if other_row else row) * 8 + at(y, dy) * 2 + (1 - core if other_core else core)
+
+    own = place(False, 0)
     loads = []
     for n, (src, dst) in enumerate(
-        ((act_h, act_v), (gate_h, gate_v), (up_h, up_v), (hid_h, hid_v), (wg_h, wg_v), (wu_h, wu_v))
+        (
+            (act_h, ag.at[own]), (gate_h, gate_v), (up_h, up_v), (hid_h, hid_v),
+            (wg_h, wp.at[0:HID]), (wu_h, wp.at[HID:WIDE]),
+        )
     ):
         loads.append(pltpu.make_async_copy(src, dst, in_sem.at[n]))
         loads[-1].start()
@@ -97,9 +96,6 @@
             device_id=mate, device_id_type=MESH,
         ).wait_recv()
 
-    def place(other_row, dy, other_core=False):
-        return (1 - row if other_row else row) * 8 + at(y, dy) * 2 + (1 - core if other_core else core)
-
     n_ag = [0]
 
     def ag_give(slot, to):
@@ -109,9 +105,7 @@
     def ag_take(slot):
         arrived(ag.at[slot], ag_recv.at[slot], ag_send.at[0])
 
-    own = place(False, 0)
     loads[0].wait()
-    ag[own] = act_v[...].T
     pl.semaphore_wait(barrier, 8)
     for to in (pair, y_up, y_down, mate):
         ag_give(own, to)
@@ -120,17 +114,19 @@
         load.wait()
 
     def gate_rows(i, carry):
-        rows = pl.ds(pl.multiple_of(i * 64, 64), 64)
-        store_packed(gp, rows, *geglu_grads(gate_v[rows, :], up_v[rows, :], hid_v[rows, :]))
+        rows = pl.ds(pl.multiple_of(i * 16, 16), 16)
+        gate_grad, up_grad = geglu_grads(gate_v[rows, :], up_v[rows, :], hid_v[rows, :])
+        gp_t[rows, :] = gate_grad
+        gp_t[pl.ds(pl.multiple_of(HID + i * 16, 16), 16), :] = up_grad
         return carry
 
-    lax.fori_loop(0, TOK // 64, gate_rows, 0)
+    lax.fori_loop(0, HID // 16, gate_rows, 0)
 
     order = ((False, 0), (True, 0), (False, -s), (False, s), (True, -s), (True, s), (False, 2), (True, 2))
 
-    def base_row(k):
+    def first_block(k):
         other_row, dy = order[k]
-        return pl.multiple_of(((1 - row if other_row else row) * 8 + at(y, dy) * 2) * COLS, CH)
+        return (1 - row if other_row else row) * 8 + at(y, dy) * 2
 
     def c_give(k, n, src, dst, to):
         send(src, dst, c_send.at[k, n], c_recv.at[k, n], to)
@@ -144,46 +140,49 @@
     def c0(k):
         other_row, dy = order[k]
         ag_take(place(other_row, dy, True))
-        first = pl.multiple_of(place(other_row, dy) - core, 2)
-        lhs = ag[pl.ds(first, 2)].reshape(CH, TOK)
-        part[k] = jnp.dot(lhs, gp[...], preferred_element_type=F32)
-        xs[k, 0] = part[k, x_rows(at(x, 2)), :].astype(BF16)
+        first = first_block(k)
+        both = jnp.concatenate([ag[first], ag[first + 1]], axis=1)
+        sums = jnp.dot(gp_t[...], both, preferred_element_type=F32)
+        part[k, 0] = sums[:, 0:COLS]
+        part[k, 1] = sums[:, COLS : 2 * COLS]
+        xs[k, 0] = part[k, :, x_rows(at(x, 2)), :].astype(BF16)
         c_give(k, 0, xs.at[k, 0], xr.at[k, 0], x_up)
-        xs[k, 1] = part[k, x_rows(at(x, -s)), :].astype(BF16)
+        xs[k, 1] = part[k, :, x_rows(at(x, -s)), :].astype(BF16)
         c_give(k, 1, xs.at[k, 1], xr.at[k, 1], x_down)
 
     def c1(k):
         c_take(k, 0, xr.at[k, 0])
-        x3[k] = (part[k, x_rows(at(x, s)), :] + xr[k, 0].astype(F32)).astype(BF16)
+        x3[k] = (part[k, :, x_rows(at(x, s)), :] + xr[k, 0].astype(F32)).astype(BF16)
         c_give(k, 2, x3.at[k], xr.at[k, 2], x_up)
 
     def c2(k):
         c_take(k, 1, xr.at[k, 1])
         c_take(k, 2, xr.at[k, 2])
-        q1[k] = part[k, x_rows(x), :] + xr[k, 1].astype(F32) + xr[k, 2].astype(F32)
-        qs[k, 0] = q1[k, z_rows(at(zh, 2)), :].astype(BF16)
+        q1[k] = part[k, :, x_rows(x), :] + xr[k, 1].astype(F32) + xr[k, 2].astype(F32)
+        qs[k, 0] = z_part(k, at(zh, 2)).astype(BF16)
         c_give(k, 3, qs.at[k, 0], zr.at[k, 0], z_up)
-        qs[k, 1] = q1[k, z_rows(at(zh, -s)), :].astype(BF16)
+        qs[k, 1] = z_part(k, at(zh, -s)).astype(BF16)
         c_give(k, 4, qs.at[k, 1], zr.at[k, 1], z_down)
 
-    def z_rows(place_z):
-        return pl.ds(pl.multiple_of(place_z * ZR, ZR), ZR)
+    def z_part(k, place_z):
+        return q1[k, place_z // 2, pl.ds(pl.multiple_of(lax.rem(place_z, 2) * ZR, ZR), ZR), :]
 
     def c3(k):
         c_take(k, 3, zr.at[k, 0])
-        z3[k] = q1[k, z_rows(at(zh, s)), :] + zr[k, 0].astype(F32)
+        z3[k] = z_part(k, at(zh, s)) + zr[k, 0].astype(F32)
         c_give(k, 5, z3.at[k], z3r.at[k], z_up)
 
     def out_x(k, place_x):
-        return w_out.at[pl.ds(pl.multiple_of(base_row(k) + place_x * XR, XR), XR), :]
+        return w_out.at[pl.ds(first_block(k), 2), x_rows(place_x), :]
 
     def out_z(k, place_z):
-        return w_out.at[pl.ds(pl.multiple_of(base_row(k) + x * XR + place_z * ZR, ZR), ZR), :]
+        rows = pl.ds(pl.multiple_of(x * XR + lax.rem(place_z, 2) * ZR, ZR), ZR)
+        return w_out.at[first_block(k) + place_z // 2, rows, :]
 
     def c4(k):
         c_take(k, 4, zr.at[k, 1])
         c_take(k, 5, z3r.at[k])
-        total = q1[k, z_rows(zh), :] + zr[k, 1].astype(F32) + z3r[k]
+        total = z_part(k, zh) + zr[k, 1].astype(F32) + z3r[k]
         mine = out_z(k, zh)
         mine[...] = total.astype(BF16)
         c_give(k, 6, mine, mine, z_up)
@@ -230,26 +229,22 @@
         ag_take(slot)
         ag_give(slot, mate)
 
-    def pack_weights():
+    def flip():
         loads[4].wait()
         loads[5].wait()
-
-        def step(i, carry):
-            rows = pl.ds(pl.multiple_of(i * 128, 128), 128)
-            store_packed(wp, rows, wg_v[rows, :], wu_v[rows, :])
-            return carry
-
-        lax.fori_loop(0, D // 128, step, 0)
+        for i in range(TOK // 128):
+            rows = slice(i * 128, i * 128 + 128)
+            gp[rows, :] = gp_t[:, rows].T
 
     def b0(i):
         first = ((i // 4) * 8 + at(y, i % 4) * 2) * COLS
-        mine = wp[pl.ds(pl.multiple_of(first + core * COLS, COLS), COLS), :]
-        others = wp[pl.ds(pl.multiple_of(first + (1 - core) * COLS, COLS), COLS), :]
-        both = jnp.concatenate([mine, others], axis=0)
+        mine = wp[:, pl.ds(pl.multiple_of(first + core * COLS, COLS), COLS)]
+        others = wp[:, pl.ds(pl.multiple_of(first + (1 - core) * COLS, COLS), COLS)]
+        both = jnp.concatenate([mine, others], axis=1)
 
         def step(r, carry):
             rows = pl.ds(pl.multiple_of(r * 256, 256), 256)
-            sums = lax.dot_general(gp[rows, :], both, NT, preferred_element_type=F32)
+            sums = jnp.dot(gp[rows, :], both, preferred_element_type=F32)
             pkeep[i, rows, :] = sums[:, 0:COLS]
             bs[i, rows, :] = sums[:, COLS : 2 * COLS].astype(BF16)
             return carry
@@ -293,7 +288,7 @@
         arrived(last_out, t_recv, t_send)
 
     extra = {
-        0: (pack_weights, lambda: b0(0), lambda: b0(1), lambda: b0(2), lambda: b0(3), ag_pair),
+        0: (flip, lambda: b0(0), lambda: b0(1), lambda: b0(2), lambda: b0(3), ag_pair),
         1: (lambda: ag_near(False), lambda: b0(4), lambda: b0(5)),
         2: (lambda: b0(6), lambda: b0(7)),
         3: (),
@@ -328,19 +323,19 @@
         kernel,
         name="exchange",
         out_shape=(
-            jax.ShapeDtypeStruct((D, WIDE), BF16),
+            jax.ShapeDtypeStruct((16, WIDE, COLS), BF16),
             jax.ShapeDtypeStruct((TOK, COLS), F32),
             jax.ShapeDtypeStruct((TOK, COLS), BF16),
         ),
         in_specs=[pl.BlockSpec(memory_space=pl.ANY)] * 6,
         out_specs=[pl.BlockSpec(memory_space=pltpu.VMEM)] * 3,
         scratch_shapes=[
-            vmem((TOK, COLS), BF16), vmem((TOK, HID), BF16), vmem((TOK, HID), BF16), vmem((TOK, HID), BF16),
-            vmem((D, HID), BF16), vmem((D, HID), BF16), vmem((D, WIDE), BF16), vmem((TOK, WIDE), BF16),
-            vmem((16, COLS, TOK), BF16),
-            vmem((CHUNKS, CH, WIDE), F32), vmem((CHUNKS, 2, XR, WIDE), BF16), vmem((CHUNKS, 3, XR, WIDE), BF16),
-            vmem((CHUNKS, XR, WIDE), BF16), vmem((CHUNKS, 2, ZR, WIDE), BF16), vmem((CHUNKS, XR, WIDE), F32),
-            vmem((CHUNKS, 2, ZR, WIDE), BF16), vmem((CHUNKS, ZR, WIDE), F32), vmem((CHUNKS, ZR, WIDE), F32),
+            vmem((HID, TOK), BF16), vmem((HID, TOK), BF16), vmem((HID, TOK), BF16),
+            vmem((WIDE, D), BF16), vmem((WIDE, TOK), BF16), vmem((TOK, WIDE), BF16), vmem((16, TOK, COLS), BF16),
+            vmem((CHUNKS, 2, WIDE, COLS), F32), vmem((CHUNKS, 2, 2, XR, COLS), BF16),
+            vmem((CHUNKS, 3, 2, XR, COLS), BF16), vmem((CHUNKS, 2, XR, COLS), BF16),
+            vmem((CHUNKS, 2, ZR, COLS), BF16), vmem((CHUNKS, 2, XR, COLS), F32),
+            vmem((CHUNKS, 2, ZR, COLS), BF16), vmem((CHUNKS, ZR, COLS), F32), vmem((CHUNKS, ZR, COLS), F32),
             vmem((8, TOK, COLS), F32), vmem((8, TOK, COLS), BF16), vmem((8, TOK, COLS), BF16),
             vmem((2, 2, TOK, COLS), F32), vmem((2, 2, TOK, COLS), BF16), vmem((2, 3, TOK, COLS), BF16),
             vmem((2, TOK, COLS), BF16), vmem((TOK, COLS), BF16),
@@ -355,11 +350,10 @@
 
 
 def finish_kernel(w_ref, own_ref, last_ref, x_ref, gate_ref, up_ref):
-    w = w_ref[...].astype(F32)
-    gate_ref[:, 0:256] = w[:, 0:256]
-    up_ref[:, 0:256] = w[:, 256:512]
-    gate_ref[:, 256:320] = w[:, 512:576]
-    up_ref[:, 256:320] = w[:, 576:640]
+    for n in range(2):
+        cols = slice(n * COLS, (n + 1) * COLS)
+        gate_ref[:, cols] = w_ref[n, 0:HID, :].astype(F32)
+        up_ref[:, cols] = w_ref[n, HID:WIDE, :].astype(F32)
     x_ref[...] = own_ref[...] + last_ref[...].astype(F32)
 
 
@@ -371,25 +365,26 @@
         grid=(steps,),
         out_shape=(
             jax.ShapeDtypeStruct((TOK, COLS), F32),
-            jax.ShapeDtypeStruct((D, HID), F32),
-            jax.ShapeDtypeStruct((D, HID), F32),
+            jax.ShapeDtypeStruct((HID, D), F32),
+            jax.ShapeDtypeStruct((HID, D), F32),
         ),
         in_specs=[
-            pl.BlockSpec((D // steps, WIDE), lambda i: (i, 0)),
+            pl.BlockSpec((2, WIDE, COLS), lambda i: (i, 0, 0)),
             pl.BlockSpec((TOK // steps, COLS), lambda i: (i, 0)),
             pl.BlockSpec((TOK // steps, COLS), lambda i: (i, 0)),
         ],
         out_specs=(
             pl.BlockSpec((TOK // steps, COLS), lambda i: (i, 0)),
-            pl.BlockSpec((D // steps, HID), lambda i: (i, 0)),
-            pl.BlockSpec((D // steps, HID), lambda i: (i, 0)),
+            pl.BlockSpec((HID, 2 * COLS), lambda i: (0, i)),
+            pl.BlockSpec((HID, 2 * COLS), lambda i: (0, i)),
         ),
         cost_estimate=pl.CostEstimate(flops=10**7, bytes_accessed=10**7, transcendentals=0),
     )(w, own, last)
 
 
-def body(*args):
-    return finish(*exchange(*args))
+def body(activations, *others):
+    input_grad, gate_t, up_t = finish(*exchange(activations, *(a.T for a in others)))
+    return input_grad, gate_t.T, up_t.T
 
 
 def solution(mesh):

time: 110 us -> 93.1 us (0.85)
  local copies, waits for them, and re-layouts: 14.8 us -> 0 us
  Pallas kernels: 93.9 us -> 91.9 us
    unnamed x13 -> x0, local copies, waits for them, and re-layouts: 9.03 us -> none
    pallas_call x2 -> x0, local copies, waits for them, and re-layouts: 5.74 us -> none  [finish(): pl.pallas_call(finish_kernel, name='finish', grid=(steps,), out_shape=(ja...]
    pallas_call x1, Pallas kernels: 87.2 us -> 85.3 us  [exchange(): pl.pallas_call(kernel, name='exchange', out_shape=(jax.ShapeDtypeStruct((...]
where the time goes in v2:
time: 93.1 us; the launch traced here: 92.5 us
  Pallas kernels  91.9 us (99%)
    pallas_call x1, Pallas kernels, exchange(): pl.pallas_call(kernel, name='exchange', out_shape=(jax.ShapeDtypeStruct((...  85.3 us
    pallas_call x1, Pallas kernels, finish(): pl.pallas_call(finish_kernel, name='finish', grid=(steps,), out_shape=(ja...  6.61 us

profile of v2, /device:TPU:2, one launch (start us, length us, event | category | flops | bytes accessed | tf_op | source)
XLA Modules:
  0.0 92.5 jit_solution(17705755346129952569)
XLA Ops:
  0.6 85.3 %exchange.1 = (bf16[16,640,128]{2,1,0:T(8,128)(2,1)}, f32[1024,128]{1,0:T(8,128)}, bf16[1024,128]{1,0:T(8,128)(2,1)}) custom-call(bf16[1024,128]{1,0:T(8,128)(2,1)} %act_h.1, bf16[320,1024]{1,0:T(8,128)(2,1)} %bitcast.11, bf16[320,1024]{1,0:T(8,128)(2,1)} %bitcast.12, bf16[320,1024]{1,0:T(8,128)(2,1)} %bitcast.13, bf16[320,2048]{1,0:T(8,128)(2,1)} %bitcast.9, ...), custom_call_target="tpu_custom_call" | custom-call | flops 5000000000 | bytes 10000000 | tf_op jit(solution)/shard_map/exchange/pallas_call | solution.py:322
  85.9 6.6 %finish.1 = (f32[1024,128]{1,0:T(8,128)}, f32[320,2048]{1,0:T(8,128)}, f32[320,2048]{1,0:T(8,128)}) custom-call(bf16[16,640,128]{2,1,0:T(8,128)(2,1)} %get-tuple-element.9.w_ref, f32[1024,128]{1,0:T(8,128)} %get-tuple-element.10.own_ref, bf16[1024,128]{1,0:T(8,128)(2,1)} %get-tuple-element.11.last_ref), custom_call_target="tpu_custom_call" | custom-call | flops 10000000 | bytes 10000000 | tf_op jit(solution)/shard_map/finish/pallas_call | solution.py:362

commit v3 on v2

--- a/solution.py
+++ b/solution.py
@@ -17,9 +17,24 @@
 WIDE = 2 * HID
 COLS = 128
 D = 2048
+STEPS = 2
 CHUNKS = 8
 XR = WIDE // 4
 ZR = XR // 2
+
+
+ORDER = (
+    ("c0", 0), ("flip",), ("ag_pair",), ("b0", 7), ("b0", 3), ("c1", 0), ("ag_nearm", 0), ("ag_nearp", 0), ("c0", 1),
+    ("b0", 4), ("c0", 3), ("c2", 0), ("b0", 6), ("c0", 2), ("b0", 1), ("c1", 3), ("c1", 1), ("ag_nearp", 1),
+    ("c3", 0), ("b0", 2), ("ag_nearm", 1), ("c1", 2), ("c0", 4), ("ag_far", 0), ("c2", 3), ("b0", 5), ("c4", 0),
+    ("c2", 1), ("c0", 6), ("c0", 5), ("ag_far", 1), ("c2", 2), ("c3", 3), ("b1", 1), ("c1", 4), ("c5", 0), ("c1", 6),
+    ("c3", 1), ("b0", 0), ("c3", 2), ("c0", 7), ("c4", 3), ("c1", 5), ("c2", 4), ("c2", 6), ("c4", 2), ("c1", 7),
+    ("c5", 3), ("c4", 1), ("b1", 0), ("c2", 5), ("c6", 0), ("c3", 6), ("b2", 1), ("c5", 2), ("c2", 7), ("c6", 3),
+    ("c5", 1), ("c3", 5), ("c3", 4), ("c7", 0), ("c6", 2), ("c4", 6), ("c6", 1), ("c3", 7), ("c4", 5), ("c4", 4),
+    ("c5", 6), ("c7", 3), ("c8", 0), ("c7", 2), ("c4", 7), ("c5", 5), ("b2", 0), ("c7", 1), ("c5", 4), ("c6", 6),
+    ("c5", 7), ("c6", 5), ("c6", 4), ("c8", 2), ("c6", 7), ("c7", 6), ("c8", 3), ("b3",), ("c7", 4), ("c7", 5),
+    ("c7", 7), ("c8", 1), ("c8", 4), ("b4",), ("c8", 6), ("c8", 5), ("c8", 7),
+)
 
 
 def geglu_grads(gate_input, up_input, hidden_grad):
@@ -215,11 +230,13 @@
         for to in (y_up, y_down, mate):
             ag_give(slot, to)
 
-    def ag_near(other_row):
+    def ag_nearm(other_row):
         slot = place(other_row, -s)
         ag_take(slot)
         ag_give(slot, y_up)
         ag_give(slot, mate)
+
+    def ag_nearp(other_row):
         slot = place(other_row, s)
         ag_take(slot)
         ag_give(slot, mate)
@@ -287,31 +304,12 @@
     def b4():
         arrived(last_out, t_recv, t_send)
 
-    extra = {
-        0: (flip, lambda: b0(0), lambda: b0(1), lambda: b0(2), lambda: b0(3), ag_pair),
-        1: (lambda: ag_near(False), lambda: b0(4), lambda: b0(5)),
-        2: (lambda: b0(6), lambda: b0(7)),
-        3: (),
-        4: (lambda: ag_near(True),),
-        5: (lambda: b1(0), lambda: b1(1)),
-        6: (lambda: ag_far(False),),
-        7: (lambda: ag_far(True),),
-        8: (lambda: b2(0), lambda: b2(1)),
-        12: (b3,),
-    }
-    stages = (c0, c1, c2, c3, c4, c5, c6, c7, c8)
-    before = {2, 4, 6, 7}
-    for t in range(CHUNKS + len(stages) - 1):
-        if t in before:
-            for f in extra.get(t, ()):
-                f()
-        for n in range(len(stages) - 1, -1, -1):
-            if 0 <= t - n < CHUNKS:
-                stages[n](t - n)
-        if t not in before:
-            for f in extra.get(t, ()):
-                f()
-    b4()
+    steps = dict(
+        c0=c0, c1=c1, c2=c2, c3=c3, c4=c4, c5=c5, c6=c6, c7=c7, c8=c8, flip=flip, b0=b0, b1=b1, b2=b2, b3=b3, b4=b4,
+        ag_pair=ag_pair, ag_nearm=ag_nearm, ag_nearp=ag_nearp, ag_far=ag_far,
+    )
+    for name, *n in ORDER:
+        steps[name](*n)
     for copy in sent:
         copy.wait_send()
 
@@ -350,7 +348,7 @@
 
 
 def finish_kernel(w_ref, own_ref, last_ref, x_ref, gate_ref, up_ref):
-    for n in range(2):
+    for n in range(16 // STEPS):
         cols = slice(n * COLS, (n + 1) * COLS)
         gate_ref[:, cols] = w_ref[n, 0:HID, :].astype(F32)
         up_ref[:, cols] = w_ref[n, HID:WIDE, :].astype(F32)
@@ -358,25 +356,24 @@
 
 
 def finish(w, own, last):
-    steps = 8
     return pl.pallas_call(
         finish_kernel,
         name="finish",
-        grid=(steps,),
+        grid=(STEPS,),
         out_shape=(
             jax.ShapeDtypeStruct((TOK, COLS), F32),
             jax.ShapeDtypeStruct((HID, D), F32),
             jax.ShapeDtypeStruct((HID, D), F32),
         ),
         in_specs=[
-            pl.BlockSpec((2, WIDE, COLS), lambda i: (i, 0, 0)),
-            pl.BlockSpec((TOK // steps, COLS), lambda i: (i, 0)),
-            pl.BlockSpec((TOK // steps, COLS), lambda i: (i, 0)),
+            pl.BlockSpec((16 // STEPS, WIDE, COLS), lambda i: (i, 0, 0)),
+            pl.BlockSpec((TOK // STEPS, COLS), lambda i: (i, 0)),
+            pl.BlockSpec((TOK // STEPS, COLS), lambda i: (i, 0)),
         ],
         out_specs=(
-            pl.BlockSpec((TOK // steps, COLS), lambda i: (i, 0)),
-            pl.BlockSpec((HID, 2 * COLS), lambda i: (0, i)),
-            pl.BlockSpec((HID, 2 * COLS), lambda i: (0, i)),
+            pl.BlockSpec((TOK // STEPS, COLS), lambda i: (i, 0)),
+            pl.BlockSpec((HID, D // STEPS), lambda i: (0, i)),
+            pl.BlockSpec((HID, D // STEPS), lambda i: (0, i)),
         ),
         cost_estimate=pl.CostEstimate(flops=10**7, bytes_accessed=10**7, transcendentals=0),
     )(w, own, last)

time: 93.1 us -> 77.9 us (0.84)
  Pallas kernels: 91.9 us -> 76.3 us
    pallas_call x1, Pallas kernels: 85.3 us -> 72.2 us  [exchange(): pl.pallas_call(kernel, name='exchange', out_shape=(jax.ShapeDtypeStruct((...]
    pallas_call x1, Pallas kernels: 6.61 us -> 4.18 us  [finish(): pl.pallas_call(finish_kernel, name='finish', grid=(STEPS,), out_shape=(ja...]
where the time goes in v3:
time: 77.9 us; the launch traced here: 77 us
  Pallas kernels  76.3 us (98%)
    pallas_call x1, Pallas kernels, exchange(): pl.pallas_call(kernel, name='exchange', out_shape=(jax.ShapeDtypeStruct((...  72.2 us
    pallas_call x1, Pallas kernels, finish(): pl.pallas_call(finish_kernel, name='finish', grid=(STEPS,), out_shape=(ja...  4.18 us

profile of v3, /device:TPU:2, one launch (start us, length us, event | category | flops | bytes accessed | tf_op | source)
XLA Modules:
  0.0 77.0 jit_solution(8048910708873993346)
XLA Ops:
  0.6 72.2 %exchange.1 = (bf16[16,640,128]{2,1,0:T(8,128)(2,1)}, f32[1024,128]{1,0:T(8,128)}, bf16[1024,128]{1,0:T(8,128)(2,1)}) custom-call(bf16[1024,128]{1,0:T(8,128)(2,1)} %act_h.1, bf16[320,1024]{1,0:T(8,128)(2,1)} %bitcast.11, bf16[320,1024]{1,0:T(8,128)(2,1)} %bitcast.12, bf16[320,1024]{1,0:T(8,128)(2,1)} %bitcast.13, bf16[320,2048]{1,0:T(8,128)(2,1)} %bitcast.9, ...), custom_call_target="tpu_custom_call" | custom-call | flops 5000000000 | bytes 10000000 | tf_op jit(solution)/shard_map/exchange/pallas_call | solution.py:320
  72.8 4.2 %finish.1 = (f32[1024,128]{1,0:T(8,128)}, f32[320,2048]{1,0:T(8,128)}, f32[320,2048]{1,0:T(8,128)}) custom-call(bf16[16,640,128]{2,1,0:T(8,128)(2,1)} %get-tuple-element.9.w_ref, f32[1024,128]{1,0:T(8,128)} %get-tuple-element.10.own_ref, bf16[1024,128]{1,0:T(8,128)(2,1)} %get-tuple-element.11.last_ref), custom_call_target="tpu_custom_call" | custom-call | flops 10000000 | bytes 10000000 | tf_op jit(solution)/shard_map/finish/pallas_call | solution.py:359

commit v4 on v3

--- a/solution.py
+++ b/solution.py
@@ -17,23 +17,27 @@
 WIDE = 2 * HID
 COLS = 128
 D = 2048
-STEPS = 2
+STEPS = 4
 CHUNKS = 8
 XR = WIDE // 4
 ZR = XR // 2
 
 
 ORDER = (
-    ("c0", 0), ("flip",), ("ag_pair",), ("b0", 7), ("b0", 3), ("c1", 0), ("ag_nearm", 0), ("ag_nearp", 0), ("c0", 1),
-    ("b0", 4), ("c0", 3), ("c2", 0), ("b0", 6), ("c0", 2), ("b0", 1), ("c1", 3), ("c1", 1), ("ag_nearp", 1),
-    ("c3", 0), ("b0", 2), ("ag_nearm", 1), ("c1", 2), ("c0", 4), ("ag_far", 0), ("c2", 3), ("b0", 5), ("c4", 0),
-    ("c2", 1), ("c0", 6), ("c0", 5), ("ag_far", 1), ("c2", 2), ("c3", 3), ("b1", 1), ("c1", 4), ("c5", 0), ("c1", 6),
-    ("c3", 1), ("b0", 0), ("c3", 2), ("c0", 7), ("c4", 3), ("c1", 5), ("c2", 4), ("c2", 6), ("c4", 2), ("c1", 7),
-    ("c5", 3), ("c4", 1), ("b1", 0), ("c2", 5), ("c6", 0), ("c3", 6), ("b2", 1), ("c5", 2), ("c2", 7), ("c6", 3),
-    ("c5", 1), ("c3", 5), ("c3", 4), ("c7", 0), ("c6", 2), ("c4", 6), ("c6", 1), ("c3", 7), ("c4", 5), ("c4", 4),
-    ("c5", 6), ("c7", 3), ("c8", 0), ("c7", 2), ("c4", 7), ("c5", 5), ("b2", 0), ("c7", 1), ("c5", 4), ("c6", 6),
-    ("c5", 7), ("c6", 5), ("c6", 4), ("c8", 2), ("c6", 7), ("c7", 6), ("c8", 3), ("b3",), ("c7", 4), ("c7", 5),
-    ("c7", 7), ("c8", 1), ("c8", 4), ("b4",), ("c8", 6), ("c8", 5), ("c8", 7),
+    ("c0", 0), ("flip",), ("b0", 5), ("ag_pair",), ("c1", 0), ("ag_nearp", 0), ("ag_nearm", 0), ("b0", 3), ("c0", 1),
+    ("c0", 2), ("b0", 0), ("c2", 0), ("c0", 3), ("c1", 1), ("b0", 4), ("b0", 6), ("b0", 1), ("ag_nearm", 1),
+    ("ag_nearp", 1), ("c4", 0), ("c1", 3), ("c1", 2), ("b0", 2), ("c2", 1), ("c0", 5), ("ag_far", 0), ("c0", 4),
+    ("zin", 0, 1), ("c2", 3), ("c8", 0, 0), ("b1", 0), ("c2", 2), ("ag_far", 1), ("c1", 5), ("c4", 1), ("b0", 7),
+    ("c0", 7), ("c4", 3), ("c1", 4), ("b1", 1), ("c2", 5), ("c4", 2), ("c0", 6), ("c1", 7), ("c8", 3, 0),
+    ("zin", 1, 1), ("b2", 0), ("c2", 4), ("c8", 2, 0), ("zin", 0, 3), ("c4", 5), ("c1", 6), ("c2", 7), ("zin", 3, 1),
+    ("c8", 0, 1), ("zin", 2, 3), ("zin", 1, 2), ("zin", 3, 2), ("zin", 0, 2), ("zin", 3, 3), ("zin", 2, 2), ("c2", 6),
+    ("zin", 1, 3), ("b2", 1), ("c8", 1, 1), ("c4", 4), ("c8", 2, 3), ("c8", 5, 0), ("c8", 3, 2), ("zin", 2, 1),
+    ("c8", 0, 3), ("zin", 5, 1), ("c8", 1, 0), ("c4", 7), ("c8", 1, 2), ("zin", 5, 2), ("c8", 0, 2), ("c4", 6),
+    ("c8", 1, 3), ("c8", 3, 1), ("c8", 2, 2), ("zin", 4, 2), ("c8", 5, 1), ("zin", 4, 3), ("c8", 2, 1), ("zin", 5, 3),
+    ("zin", 7, 2), ("c8", 6, 0), ("zin", 4, 1), ("zin", 7, 3), ("b3",), ("zin", 6, 1), ("c8", 7, 0), ("zin", 6, 3),
+    ("zin", 7, 1), ("zin", 6, 2), ("c8", 4, 0), ("c8", 4, 1), ("c8", 3, 3), ("c8", 5, 2), ("c8", 7, 3), ("c8", 4, 2),
+    ("c8", 4, 3), ("c8", 5, 3), ("c8", 6, 3), ("c9", 2), ("c9", 0), ("c8", 7, 1), ("c8", 7, 2), ("c9", 1),
+    ("c8", 6, 1), ("c8", 6, 2), ("c9", 4), ("c9", 5), ("c9", 3), ("c9", 7), ("c9", 6), ("b4",),
 )
 
 
@@ -51,11 +55,12 @@
 
 def kernel(
     act_h, gate_h, up_h, hid_h, wg_h, wu_h,
-    w_out, own_out, last_out,
+    w_hbm, own_out, last_out,
+    w_out,
     gate_v, up_v, hid_v, wp, gp_t, gp, ag,
-    part, xs, xr, x3, qs, q1, zr, z3, z3r,
+    part, xs, xr, x3, qs, q1, zr,
     pkeep, bs, br, ykeep, ys, yr, y3, tz,
-    in_sem, ag_recv, ag_send, c_recv, c_send, b_recv, b_send, y_recv, y_send, t_recv, t_send,
+    in_sem, out_sem, ag_recv, ag_send, c_recv, c_send, b_recv, b_send, y_recv, y_send, t_recv, t_send,
 ):
     dp, row, col = lax.axis_index("dp"), lax.axis_index("row"), lax.axis_index("col")
     zh, x = dp // 4, lax.rem(dp, 4)
@@ -75,6 +80,7 @@
     x_up, x_down = dev(dx=s), dev(dx=-s)
     z_up, z_down = dev(dzh=s), dev(dzh=-s)
     y_up, y_down = dev(dy=s), dev(dy=-s)
+    z_far = dev(dzh=2)
     pair, mate = dev(flip_row=True), dev(flip_core=True)
 
     def place(other_row, dy, other_core=False):
@@ -92,7 +98,7 @@
         loads[-1].start()
 
     barrier = pltpu.get_barrier_semaphore()
-    for other in (x_up, x_down, z_up, z_down, y_up, y_down, pair, mate):
+    for other in (x_up, x_down, z_up, z_down, z_far, y_up, y_down, pair, mate):
         pl.semaphore_signal(barrier, inc=1, device_id=other, device_id_type=MESH)
 
     sent = []
@@ -121,7 +127,7 @@
         arrived(ag.at[slot], ag_recv.at[slot], ag_send.at[0])
 
     loads[0].wait()
-    pl.semaphore_wait(barrier, 8)
+    pl.semaphore_wait(barrier, 9)
     for to in (pair, y_up, y_down, mate):
         ag_give(own, to)
 
@@ -174,55 +180,52 @@
         c_take(k, 1, xr.at[k, 1])
         c_take(k, 2, xr.at[k, 2])
         q1[k] = part[k, :, x_rows(x), :] + xr[k, 1].astype(F32) + xr[k, 2].astype(F32)
-        qs[k, 0] = z_part(k, at(zh, 2)).astype(BF16)
-        c_give(k, 3, qs.at[k, 0], zr.at[k, 0], z_up)
-        qs[k, 1] = z_part(k, at(zh, -s)).astype(BF16)
-        c_give(k, 4, qs.at[k, 1], zr.at[k, 1], z_down)
+        for n, (step, to) in enumerate(((2, z_far), (-s, z_down), (s, z_up))):
+            qs[k, n] = z_part(k, at(zh, step)).astype(BF16)
+            c_give(k, 3 + n, qs.at[k, n], zr.at[k, n], to)
 
     def z_part(k, place_z):
         return q1[k, place_z // 2, pl.ds(pl.multiple_of(lax.rem(place_z, 2) * ZR, ZR), ZR), :]
 
-    def c3(k):
-        c_take(k, 3, zr.at[k, 0])
-        z3[k] = z_part(k, at(zh, s)) + zr[k, 0].astype(F32)
-        c_give(k, 5, z3.at[k], z3r.at[k], z_up)
-
-    def out_x(k, place_x):
-        return w_out.at[pl.ds(first_block(k), 2), x_rows(place_x), :]
-
-    def out_z(k, place_z):
-        rows = pl.ds(pl.multiple_of(x * XR + lax.rem(place_z, 2) * ZR, ZR), ZR)
+    def out_part(k, place_x, place_z):
+        rows = pl.ds(pl.multiple_of(place_x * XR + lax.rem(place_z, 2) * ZR, ZR), ZR)
         return w_out.at[first_block(k) + place_z // 2, rows, :]
 
+    z_from = (0, -s, s, 2)
+
     def c4(k):
-        c_take(k, 4, zr.at[k, 1])
-        c_take(k, 5, z3r.at[k])
-        total = z_part(k, zh) + zr[k, 1].astype(F32) + z3r[k]
-        mine = out_z(k, zh)
+        for n in range(3):
+            c_take(k, 3 + n, zr.at[k, n])
+        total = z_part(k, zh) + zr[k, 0].astype(F32) + zr[k, 1].astype(F32) + zr[k, 2].astype(F32)
+        mine = out_part(k, x, zh)
         mine[...] = total.astype(BF16)
-        c_give(k, 6, mine, mine, z_up)
-        c_give(k, 7, mine, mine, z_down)
-
-    def c5(k):
-        got = out_z(k, at(zh, -s))
-        c_take(k, 6, got)
-        c_give(k, 8, got, got, z_up)
-
-    def c6(k):
-        c_take(k, 7, out_z(k, at(zh, s)))
-        c_take(k, 8, out_z(k, at(zh, 2)))
-        mine = out_x(k, x)
-        c_give(k, 9, mine, mine, x_up)
-        c_give(k, 10, mine, mine, x_down)
-
-    def c7(k):
-        got = out_x(k, at(x, -s))
-        c_take(k, 9, got)
-        c_give(k, 11, got, got, x_up)
-
-    def c8(k):
-        c_take(k, 10, out_x(k, at(x, s)))
-        c_take(k, 11, out_x(k, at(x, 2)))
+        for n, to in enumerate((z_up, z_down, z_far)):
+            c_give(k, 6 + n, mine, mine, to)
+        along_x(k, 0)
+
+    def along_x(k, j):
+        held = out_part(k, x, at(zh, z_from[j]))
+        c_give(k, 9 + j, held, held, x_up)
+        c_give(k, 13 + j, held, held, x_down)
+
+    def z_part_in(k, j):
+        c_take(k, 5 + j, out_part(k, x, at(zh, z_from[j])))
+        along_x(k, j)
+
+    def c8(k, j):
+        got = out_part(k, at(x, -s), at(zh, z_from[j]))
+        c_take(k, 9 + j, got)
+        c_give(k, 17 + j, got, got, x_up)
+
+    def save(k):
+        pair_of = pl.ds(first_block(k), 2)
+        return pltpu.make_async_copy(w_out.at[pair_of], w_hbm.at[pair_of], out_sem.at[k])
+
+    def c9(k):
+        for j in range(4):
+            c_take(k, 13 + j, out_part(k, at(x, s), at(zh, z_from[j])))
+            c_take(k, 17 + j, out_part(k, at(x, 2), at(zh, z_from[j])))
+        save(k).start()
 
     def ag_pair():
         slot = place(True, 0)
@@ -305,13 +308,15 @@
         arrived(last_out, t_recv, t_send)
 
     steps = dict(
-        c0=c0, c1=c1, c2=c2, c3=c3, c4=c4, c5=c5, c6=c6, c7=c7, c8=c8, flip=flip, b0=b0, b1=b1, b2=b2, b3=b3, b4=b4,
+        c0=c0, c1=c1, c2=c2, c4=c4, zin=z_part_in, c8=c8, c9=c9, flip=flip, b0=b0, b1=b1, b2=b2, b3=b3, b4=b4,
         ag_pair=ag_pair, ag_nearm=ag_nearm, ag_nearp=ag_nearp, ag_far=ag_far,
     )
     for name, *n in ORDER:
         steps[name](*n)
     for copy in sent:
         copy.wait_send()
+    for k in range(CHUNKS):
+        save(k).wait()
 
 
 def exchange(*args):
@@ -326,18 +331,19 @@
             jax.ShapeDtypeStruct((TOK, COLS), BF16),
         ),
         in_specs=[pl.BlockSpec(memory_space=pl.ANY)] * 6,
-        out_specs=[pl.BlockSpec(memory_space=pltpu.VMEM)] * 3,
+        out_specs=[pl.BlockSpec(memory_space=pl.ANY)] + [pl.BlockSpec(memory_space=pltpu.VMEM)] * 2,
         scratch_shapes=[
+            vmem((16, WIDE, COLS), BF16),
             vmem((HID, TOK), BF16), vmem((HID, TOK), BF16), vmem((HID, TOK), BF16),
             vmem((WIDE, D), BF16), vmem((WIDE, TOK), BF16), vmem((TOK, WIDE), BF16), vmem((16, TOK, COLS), BF16),
             vmem((CHUNKS, 2, WIDE, COLS), F32), vmem((CHUNKS, 2, 2, XR, COLS), BF16),
             vmem((CHUNKS, 3, 2, XR, COLS), BF16), vmem((CHUNKS, 2, XR, COLS), BF16),
-            vmem((CHUNKS, 2, ZR, COLS), BF16), vmem((CHUNKS, 2, XR, COLS), F32),
-            vmem((CHUNKS, 2, ZR, COLS), BF16), vmem((CHUNKS, ZR, COLS), F32), vmem((CHUNKS, ZR, COLS), F32),
+            vmem((CHUNKS, 3, ZR, COLS), BF16), vmem((CHUNKS, 2, XR, COLS), F32),
+            vmem((CHUNKS, 3, ZR, COLS), BF16),
             vmem((8, TOK, COLS), F32), vmem((8, TOK, COLS), BF16), vmem((8, TOK, COLS), BF16),
             vmem((2, 2, TOK, COLS), F32), vmem((2, 2, TOK, COLS), BF16), vmem((2, 3, TOK, COLS), BF16),
             vmem((2, TOK, COLS), BF16), vmem((TOK, COLS), BF16),
-            dma((6,)), dma((16,)), dma((16,)), dma((CHUNKS, 12)), dma((CHUNKS, 12)), dma((8,)), dma((8,)),
+            dma((6,)), dma((CHUNKS,)), dma((16,)), dma((16,)), dma((CHUNKS, 21)), dma((CHUNKS, 21)), dma((8,)), dma((8,)),
             dma((2, 3)), dma((2, 3)), dma, dma,
         ],
         compiler_params=pltpu.CompilerParams(
@@ -347,34 +353,57 @@
     )(*args)
 
 
-def finish_kernel(w_ref, own_ref, last_ref, x_ref, gate_ref, up_ref):
-    for n in range(16 // STEPS):
-        cols = slice(n * COLS, (n + 1) * COLS)
-        gate_ref[:, cols] = w_ref[n, 0:HID, :].astype(F32)
-        up_ref[:, cols] = w_ref[n, HID:WIDE, :].astype(F32)
-    x_ref[...] = own_ref[...] + last_ref[...].astype(F32)
+def finish_kernel(
+    w_h, own_h, last_h, x_h, gate_h, up_h, w_v, own_v, last_v, x_v, gate_v, up_v, in_sem, x_sem, out_sem
+):
+    wide = D // STEPS
+    loads = []
+    for i in range(STEPS):
+        blocks = slice(i * (16 // STEPS), (i + 1) * (16 // STEPS))
+        loads.append(pltpu.make_async_copy(w_h.at[blocks], w_v.at[blocks], in_sem.at[i]))
+    loads.append(pltpu.make_async_copy(own_h, own_v, x_sem.at[0]))
+    loads.append(pltpu.make_async_copy(last_h, last_v, x_sem.at[1]))
+    for load in loads:
+        load.start()
+    stores = []
+    for i in range(STEPS):
+        loads[i].wait()
+        for b in range(i * (16 // STEPS), (i + 1) * (16 // STEPS)):
+            cols = slice(b * COLS, (b + 1) * COLS)
+            gate_v[:, cols] = w_v[b, 0:HID, :].astype(F32)
+            up_v[:, cols] = w_v[b, HID:WIDE, :].astype(F32)
+        cols = slice(i * wide, (i + 1) * wide)
+        stores.append(pltpu.make_async_copy(gate_v.at[:, cols], gate_h.at[:, cols], out_sem.at[2 * i]))
+        stores.append(pltpu.make_async_copy(up_v.at[:, cols], up_h.at[:, cols], out_sem.at[2 * i + 1]))
+        stores[-2].start()
+        stores[-1].start()
+    loads[-2].wait()
+    loads[-1].wait()
+    x_v[...] = own_v[...] + last_v[...].astype(F32)
+    stores.append(pltpu.make_async_copy(x_v, x_h, x_sem.at[2]))
+    stores[-1].start()
+    for store in stores:
+        store.wait()
 
 
 def finish(w, own, last):
+    vmem = pltpu.VMEM
     return pl.pallas_call(
         finish_kernel,
         name="finish",
-        grid=(STEPS,),
         out_shape=(
             jax.ShapeDtypeStruct((TOK, COLS), F32),
             jax.ShapeDtypeStruct((HID, D), F32),
             jax.ShapeDtypeStruct((HID, D), F32),
         ),
-        in_specs=[
-            pl.BlockSpec((16 // STEPS, WIDE, COLS), lambda i: (i, 0, 0)),
-            pl.BlockSpec((TOK // STEPS, COLS), lambda i: (i, 0)),
-            pl.BlockSpec((TOK // STEPS, COLS), lambda i: (i, 0)),
+        in_specs=[pl.BlockSpec(memory_space=pl.ANY)] * 3,
+        out_specs=[pl.BlockSpec(memory_space=pl.ANY)] * 3,
+        scratch_shapes=[
+            vmem((16, WIDE, COLS), BF16), vmem((TOK, COLS), F32), vmem((TOK, COLS), BF16), vmem((TOK, COLS), F32),
+            vmem((HID, D), F32), vmem((HID, D), F32),
+            pltpu.SemaphoreType.DMA((STEPS,)), pltpu.SemaphoreType.DMA((3,)), pltpu.SemaphoreType.DMA((2 * STEPS,)),
         ],
-        out_specs=(
-            pl.BlockSpec((TOK // STEPS, COLS), lambda i: (i, 0)),
-            pl.BlockSpec((HID, D // STEPS), lambda i: (0, i)),
-            pl.BlockSpec((HID, D // STEPS), lambda i: (0, i)),
-        ),
+        compiler_params=pltpu.CompilerParams(vmem_limit_bytes=63 * 1024 * 1024),
         cost_estimate=pl.CostEstimate(flops=10**7, bytes_accessed=10**7, transcendentals=0),
     )(w, own, last)
 

time: 77.9 us -> 75.5 us (0.969); the launches traced: 77 us -> 75.4 us
  Pallas kernels: 76.3 us -> 74.8 us
    pallas_call x1, Pallas kernels: 72.2 us -> 71 us  [exchange(): pl.pallas_call(kernel, name='exchange', out_shape=(jax.ShapeDtypeStruct((...]
where the time goes in v4:
time: 75.5 us; the launch traced here: 75.4 us
  Pallas kernels  74.8 us (99%)
    pallas_call x1, Pallas kernels, exchange(): pl.pallas_call(kernel, name='exchange', out_shape=(jax.ShapeDtypeStruct((...  71 us
    pallas_call x1, Pallas kernels, finish(): pl.pallas_call(finish_kernel, name='finish', out_shape=(jax.ShapeDtypeStr...  3.8 us

profile of v4, /device:TPU:2, one launch (start us, length us, event | category | flops | bytes accessed | tf_op | source)
XLA Modules:
  0.0 75.4 jit_solution(13116712850991244361)
XLA Ops:
  0.6 71.0 %exchange.1 = (bf16[16,640,128]{2,1,0:T(8,128)(2,1)}, f32[1024,128]{1,0:T(8,128)}, bf16[1024,128]{1,0:T(8,128)(2,1)}) custom-call(bf16[1024,128]{1,0:T(8,128)(2,1)} %act_h.1, bf16[320,1024]{1,0:T(8,128)(2,1)} %bitcast.11, bf16[320,1024]{1,0:T(8,128)(2,1)} %bitcast.12, bf16[320,1024]{1,0:T(8,128)(2,1)} %bitcast.13, bf16[320,2048]{1,0:T(8,128)(2,1)} %bitcast.9, ...), custom_call_target="tpu_custom_call" | custom-call | flops 5000000000 | bytes 10000000 | tf_op jit(solution)/shard_map/exchange/pallas_call | solution.py:325
  71.6 3.8 %finish.1 = (f32[1024,128]{1,0:T(8,128)}, f32[320,2048]{1,0:T(8,128)}, f32[320,2048]{1,0:T(8,128)}) custom-call(bf16[16,640,128]{2,1,0:T(8,128)(2,1)} %get-tuple-element.9.w_h, f32[1024,128]{1,0:T(8,128)} %get-tuple-element.10.own_h, bf16[1024,128]{1,0:T(8,128)(2,1)} %get-tuple-element.11.last_h), custom_call_target="tpu_custom_call" | custom-call | flops 10000000 | bytes 10000000 | tf_op jit(solution)/shard_map/finish/pallas_call | solution.py:391

commit v5 on v4

--- a/solution.py
+++ b/solution.py
@@ -17,27 +17,27 @@
 WIDE = 2 * HID
 COLS = 128
 D = 2048
-STEPS = 4
+STEPS = 8
 CHUNKS = 8
 XR = WIDE // 4
 ZR = XR // 2
 
 
 ORDER = (
-    ("c0", 0), ("flip",), ("b0", 5), ("ag_pair",), ("c1", 0), ("ag_nearp", 0), ("ag_nearm", 0), ("b0", 3), ("c0", 1),
-    ("c0", 2), ("b0", 0), ("c2", 0), ("c0", 3), ("c1", 1), ("b0", 4), ("b0", 6), ("b0", 1), ("ag_nearm", 1),
-    ("ag_nearp", 1), ("c4", 0), ("c1", 3), ("c1", 2), ("b0", 2), ("c2", 1), ("c0", 5), ("ag_far", 0), ("c0", 4),
-    ("zin", 0, 1), ("c2", 3), ("c8", 0, 0), ("b1", 0), ("c2", 2), ("ag_far", 1), ("c1", 5), ("c4", 1), ("b0", 7),
-    ("c0", 7), ("c4", 3), ("c1", 4), ("b1", 1), ("c2", 5), ("c4", 2), ("c0", 6), ("c1", 7), ("c8", 3, 0),
-    ("zin", 1, 1), ("b2", 0), ("c2", 4), ("c8", 2, 0), ("zin", 0, 3), ("c4", 5), ("c1", 6), ("c2", 7), ("zin", 3, 1),
-    ("c8", 0, 1), ("zin", 2, 3), ("zin", 1, 2), ("zin", 3, 2), ("zin", 0, 2), ("zin", 3, 3), ("zin", 2, 2), ("c2", 6),
-    ("zin", 1, 3), ("b2", 1), ("c8", 1, 1), ("c4", 4), ("c8", 2, 3), ("c8", 5, 0), ("c8", 3, 2), ("zin", 2, 1),
-    ("c8", 0, 3), ("zin", 5, 1), ("c8", 1, 0), ("c4", 7), ("c8", 1, 2), ("zin", 5, 2), ("c8", 0, 2), ("c4", 6),
-    ("c8", 1, 3), ("c8", 3, 1), ("c8", 2, 2), ("zin", 4, 2), ("c8", 5, 1), ("zin", 4, 3), ("c8", 2, 1), ("zin", 5, 3),
-    ("zin", 7, 2), ("c8", 6, 0), ("zin", 4, 1), ("zin", 7, 3), ("b3",), ("zin", 6, 1), ("c8", 7, 0), ("zin", 6, 3),
-    ("zin", 7, 1), ("zin", 6, 2), ("c8", 4, 0), ("c8", 4, 1), ("c8", 3, 3), ("c8", 5, 2), ("c8", 7, 3), ("c8", 4, 2),
-    ("c8", 4, 3), ("c8", 5, 3), ("c8", 6, 3), ("c9", 2), ("c9", 0), ("c8", 7, 1), ("c8", 7, 2), ("c9", 1),
-    ("c8", 6, 1), ("c8", 6, 2), ("c9", 4), ("c9", 5), ("c9", 3), ("c9", 7), ("c9", 6), ("b4",),
+    ("c0", 0), ("flip",), ("c1", 0), ("ag_nearp", 0), ("ag_pair",), ("b0", 3), ("ag_nearm", 0), ("b0", 1), ("c0", 2),
+    ("b0", 0), ("c2", 0), ("c0", 3), ("c0", 1), ("b0", 5), ("b0", 2), ("c1", 2), ("c1", 3), ("c4", 0),
+    ("ag_nearm", 1), ("c1", 1), ("ag_nearp", 1), ("c0", 5), ("c2", 2), ("b0", 7), ("c2", 3), ("c0", 4), ("zin", 0, 2),
+    ("ag_far", 0), ("b1", 0), ("c2", 1), ("b0", 6), ("c1", 5), ("ag_far", 1), ("b0", 4), ("c0", 6), ("c4", 2),
+    ("zin", 0, 1), ("c0", 7), ("c1", 4), ("c2", 5), ("b1", 1), ("zin", 0, 3), ("c4", 1), ("c4", 3), ("c1", 7),
+    ("c1", 6), ("zin", 2, 1), ("c8", 0, 0), ("c4", 5), ("c2", 4), ("zin", 3, 1), ("zin", 3, 2), ("zin", 3, 3),
+    ("c2", 7), ("zin", 2, 3), ("zin", 5, 2), ("b2", 1), ("c8", 0, 1), ("zin", 5, 3), ("c2", 6), ("zin", 1, 1),
+    ("zin", 5, 1), ("c8", 0, 3), ("c8", 3, 1), ("zin", 2, 2), ("c4", 4), ("c8", 2, 1), ("zin", 1, 3), ("c8", 3, 3),
+    ("b2", 0), ("c8", 3, 2), ("c4", 7), ("c8", 5, 3), ("c8", 1, 0), ("c8", 3, 0), ("c8", 5, 2), ("zin", 1, 2),
+    ("c4", 6), ("c8", 0, 2), ("c8", 2, 2), ("zin", 4, 2), ("c8", 2, 3), ("c8", 7, 0), ("c8", 5, 0), ("zin", 4, 1),
+    ("c8", 4, 0), ("zin", 7, 2), ("zin", 4, 3), ("b3",), ("c8", 1, 1), ("zin", 7, 3), ("zin", 7, 1), ("c9", 3),
+    ("zin", 6, 2), ("zin", 6, 1), ("c8", 5, 1), ("zin", 6, 3), ("c8", 1, 3), ("c8", 4, 1), ("c8", 6, 0), ("c8", 4, 2),
+    ("c8", 7, 2), ("c8", 2, 0), ("c9", 0), ("c8", 7, 3), ("c8", 1, 2), ("c8", 6, 2), ("c8", 4, 3), ("c8", 6, 1),
+    ("c8", 7, 1), ("c8", 6, 3), ("b4",), ("c9", 5), ("c9", 2), ("c9", 4), ("c9", 7), ("c9", 1), ("c9", 6),
 )
 
 
@@ -126,11 +126,6 @@
     def ag_take(slot):
         arrived(ag.at[slot], ag_recv.at[slot], ag_send.at[0])
 
-    loads[0].wait()
-    pl.semaphore_wait(barrier, 9)
-    for to in (pair, y_up, y_down, mate):
-        ag_give(own, to)
-
     for load in loads[1:4]:
         load.wait()
 
@@ -141,7 +136,14 @@
         gp_t[pl.ds(pl.multiple_of(HID + i * 16, 16), 16), :] = up_grad
         return carry
 
-    lax.fori_loop(0, HID // 16, gate_rows, 0)
+    lax.fori_loop(0, HID // 32, gate_rows, 0)
+
+    loads[0].wait()
+    pl.semaphore_wait(barrier, 9)
+    for to in (pair, y_up, y_down, mate):
+        ag_give(own, to)
+
+    lax.fori_loop(HID // 32, HID // 16, gate_rows, 0)
 
     order = ((False, 0), (True, 0), (False, -s), (False, s), (True, -s), (True, s), (False, 2), (True, 2))
 

time: 75.5 us -> 75.2 us (level)
  Pallas kernels: 74.8 us -> 74 us
    pallas_call x1, Pallas kernels: 71 us -> 70.2 us  [exchange(): pl.pallas_call(kernel, name='exchange', out_shape=(jax.ShapeDtypeStruct((...]
where the time goes in v5:
time: 75.2 us; the launch traced here: 74.6 us
  Pallas kernels  74 us (98%)
    pallas_call x1, Pallas kernels, exchange(): pl.pallas_call(kernel, name='exchange', out_shape=(jax.ShapeDtypeStruct((...  70.2 us
    pallas_call x1, Pallas kernels, finish(): pl.pallas_call(finish_kernel, name='finish', out_shape=(jax.ShapeDtypeStr...  3.74 us

profile of v5, /device:TPU:2, one launch (start us, length us, event | category | flops | bytes accessed | tf_op | source)
XLA Modules:
  0.0 74.6 jit_solution(2806973451543331734)
XLA Ops:
  0.6 70.2 %exchange.1 = (bf16[16,640,128]{2,1,0:T(8,128)(2,1)}, f32[1024,128]{1,0:T(8,128)}, bf16[1024,128]{1,0:T(8,128)(2,1)}) custom-call(bf16[1024,128]{1,0:T(8,128)(2,1)} %act_h.1, bf16[320,1024]{1,0:T(8,128)(2,1)} %bitcast.11, bf16[320,1024]{1,0:T(8,128)(2,1)} %bitcast.12, bf16[320,1024]{1,0:T(8,128)(2,1)} %bitcast.13, bf16[320,2048]{1,0:T(8,128)(2,1)} %bitcast.9, ...), custom_call_target="tpu_custom_call" | custom-call | flops 5000000000 | bytes 10000000 | tf_op jit(solution)/shard_map/exchange/pallas_call | solution.py:327
  70.9 3.7 %finish.1 = (f32[1024,128]{1,0:T(8,128)}, f32[320,2048]{1,0:T(8,128)}, f32[320,2048]{1,0:T(8,128)}) custom-call(bf16[16,640,128]{2,1,0:T(8,128)(2,1)} %get-tuple-element.9.w_h, f32[1024,128]{1,0:T(8,128)} %get-tuple-element.10.own_h, bf16[1024,128]{1,0:T(8,128)(2,1)} %get-tuple-element.11.last_h), custom_call_target="tpu_custom_call" | custom-call | flops 10000000 | bytes 10000000 | tf_op jit(solution)/shard_map/finish/pallas_call | solution.py:393

commit v6 on v5

--- a/solution.py
+++ b/solution.py
@@ -95,7 +95,8 @@
         )
     ):
         loads.append(pltpu.make_async_copy(src, dst, in_sem.at[n]))
-        loads[-1].start()
+        if n < 4:
+            loads[-1].start()
 
     barrier = pltpu.get_barrier_semaphore()
     for other in (x_up, x_down, z_up, z_down, z_far, y_up, y_down, pair, mate):
@@ -142,6 +143,8 @@
     pl.semaphore_wait(barrier, 9)
     for to in (pair, y_up, y_down, mate):
         ag_give(own, to)
+    for load in loads[4:]:
+        load.start()
 
     lax.fori_loop(HID // 32, HID // 16, gate_rows, 0)
 

time: 75.2 us -> 75.3 us (level)
  no operation moved by 1% of the time
where the time goes in v6:
time: 75.3 us; the launch traced here: 75.1 us
  Pallas kernels  74.5 us (99%)
    pallas_call x1, Pallas kernels, exchange(): pl.pallas_call(kernel, name='exchange', out_shape=(jax.ShapeDtypeStruct((...  70.7 us
    pallas_call x1, Pallas kernels, finish(): pl.pallas_call(finish_kernel, name='finish', out_shape=(jax.ShapeDtypeStr...  3.74 us

profile of v6, /device:TPU:2, one launch (start us, length us, event | category | flops | bytes accessed | tf_op | source)
XLA Modules:
  0.0 75.1 jit_solution(5424226163615746737)
XLA Ops:
  0.6 70.7 %exchange.1 = (bf16[16,640,128]{2,1,0:T(8,128)(2,1)}, f32[1024,128]{1,0:T(8,128)}, bf16[1024,128]{1,0:T(8,128)(2,1)}) custom-call(bf16[1024,128]{1,0:T(8,128)(2,1)} %act_h.1, bf16[320,1024]{1,0:T(8,128)(2,1)} %bitcast.11, bf16[320,1024]{1,0:T(8,128)(2,1)} %bitcast.12, bf16[320,1024]{1,0:T(8,128)(2,1)} %bitcast.13, bf16[320,2048]{1,0:T(8,128)(2,1)} %bitcast.9, ...), custom_call_target="tpu_custom_call" | custom-call | flops 5000000000 | bytes 10000000 | tf_op jit(solution)/shard_map/exchange/pallas_call | solution.py:330
  71.4 3.7 %finish.1 = (f32[1024,128]{1,0:T(8,128)}, f32[320,2048]{1,0:T(8,128)}, f32[320,2048]{1,0:T(8,128)}) custom-call(bf16[16,640,128]{2,1,0:T(8,128)(2,1)} %get-tuple-element.9.w_h, f32[1024,128]{1,0:T(8,128)} %get-tuple-element.10.own_h, bf16[1024,128]{1,0:T(8,128)(2,1)} %get-tuple-element.11.last_h), custom_call_target="tpu_custom_call" | custom-call | flops 10000000 | bytes 10000000 | tf_op jit(solution)/shard_map/finish/pallas_call | solution.py:396
